TPU v7x, 32 devices: a whole 2x2x4 slice. The times are simulated.
32 devices in a mesh: seq: 4 (over y, x), fsdp: 8 (over z, core).
Axes of the slice: x: 2, y: 2, z: 4, core: 2. Of those that a mesh axis runs over, the one named last changes fastest.
Arguments:
- images: bfloat16 [24, 512, 1152], P('fsdp', 'seq'), may hold values from -6 to 6
- key_mask: int32 [24, 512], P('fsdp'), may hold values from 0 to 1, as said below
- attn_gain: bfloat16 [1152], P('fsdp'), may hold values from 0.25 to 1.75
- attn_shift: bfloat16 [1152], P('fsdp'), may hold values from -3 to 3
- query_weight: bfloat16 [1152, 1152], P('fsdp'), may hold values from -0.1875 to 0.1875
- key_weight: bfloat16 [1152, 1152], P('fsdp'), may hold values from -0.1875 to 0.1875
- value_weight: bfloat16 [1152, 1152], P('fsdp'), may hold values from -0.1875 to 0.1875
- query_bias: bfloat16 [1152], P('fsdp'), may hold values from -3 to 3
- value_bias: bfloat16 [1152], P('fsdp'), may hold values from -0.1796875 to 0.1796875
- out_weight: bfloat16 [1152, 1152], P('fsdp'), may hold values from -1.5 to 1.5
- out_bias: bfloat16 [1152], P('fsdp'), may hold values from -3 to 3
- mlp_gain: bfloat16 [1152], P('fsdp'), may hold values from 0.25 to 1.75
- mlp_shift: bfloat16 [1152], P('fsdp'), may hold values from -3 to 3
- inner_weight: bfloat16 [1152, 4304], P('fsdp'), may hold values from -0.1875 to 0.1875
- inner_bias: bfloat16 [4304], P('fsdp'), may hold values from -3 to 3
- outer_weight: bfloat16 [4304, 1152], P('fsdp'), may hold values from -0.09375 to 0.09375
- outer_bias: bfloat16 [1152], P('fsdp'), may hold values from -3 to 3
- cotangent: bfloat16 [24, 512, 1152], P('fsdp', 'seq'), may hold values from -6 to 6
Outputs:
- layer_out: float32 [24, 512, 1152], P('fsdp', 'seq')
- images_grad: float32 [24, 512, 1152], P('fsdp', 'seq')
- attn_gain_grad: float32 [1152], P('fsdp')
- attn_shift_grad: float32 [1152], P('fsdp')
- query_weight_grad: float32 [1152, 1152], P('fsdp')
- key_weight_grad: float32 [1152, 1152], P('fsdp')
- value_weight_grad: float32 [1152, 1152], P('fsdp')
- query_bias_grad: float32 [1152], P('fsdp')
- value_bias_grad: float32 [1152], P('fsdp')
- out_weight_grad: float32 [1152, 1152], P('fsdp')
- out_bias_grad: float32 [1152], P('fsdp')
- mlp_gain_grad: float32 [1152], P('fsdp')
- mlp_shift_grad: float32 [1152], P('fsdp')
- inner_weight_grad: float32 [1152, 4304], P('fsdp')
- inner_bias_grad: float32 [4304], P('fsdp')
- outer_weight_grad: float32 [4304, 1152], P('fsdp')
- outer_bias_grad: float32 [1152], P('fsdp')
Inputs may be any that keep to these rules, and one draw needn't show every extreme that they name: `key_mask`: each image's row is 1 on its first positions and 0 after them; at least 128 positions are 1.
All inputs are finite; a program needn't handle non-finite values.
Results may differ from a plain program's by a relative error of at most 0.013.
The roundings to bfloat16 on the way count: a program that leaves them out, or rounds other values in their place, can miss the bound.
Values may be sent and summed in bfloat16 or wider, within the bound.
A program may use at most 256 MiB of HBM per device.

v0:
```python
import jax
import jax.numpy as jnp
from jax import lax
from jax.sharding import PartitionSpec as P

HD = 72
EPSILON = 1e-06
MASKED = -1e30


def product(left, right):
    return jnp.dot(left, right, preferred_element_type=jnp.float32)


def product_rows(left, right):
    return lax.dot_general(
        left, right, (((0,), (0,)), ((), ())), preferred_element_type=jnp.float32
    )


def product_back(left, right):
    return lax.dot_general(
        left, right, (((1,), (1,)), ((), ())), preferred_element_type=jnp.float32
    )


def gelu_tanh(values):
    return jax.nn.gelu(values, approximate=True)


def normalize(values):
    center = values - jnp.mean(values, axis=-1, keepdims=True)
    factor = lax.rsqrt(jnp.mean(center * center, axis=-1, keepdims=True) + EPSILON)
    return (center * factor, factor)


def norm_back(grad_normed, normed, factor):
    first = jnp.mean(grad_normed, axis=-1, keepdims=True)
    second = jnp.mean(grad_normed * normed, axis=-1, keepdims=True)
    return factor * (grad_normed - first - normed * second)


def forward_image(items):
    query, keys, values, valid = items
    length, local = query.shape
    heads = local // HD
    scale = HD ** (-0.5)
    block = min(512, length)
    key_three = keys.reshape(length, heads, HD)
    value_three = values.reshape(length, heads, HD)
    blocks = query.reshape(length // block, block, heads, HD)

    def forward_visit(query_block):
        scores = (
            jnp.einsum("qhd,khd->hqk", query_block, key_three, preferred_element_type=jnp.float32)
            * scale
        )
        scores = jnp.where(valid[None, None, :], scores, MASKED)
        highest = jnp.max(scores, axis=-1, keepdims=True)
        logsum = highest + jnp.log(jnp.sum(jnp.exp(scores - highest), axis=-1, keepdims=True))
        attention = jnp.exp(scores - logsum).astype(jnp.bfloat16)
        attended = jnp.einsum(
            "hqk,khd->qhd", attention, value_three, preferred_element_type=jnp.float32
        )
        return (attended.astype(jnp.bfloat16), logsum[..., 0])

    attended, logsum = lax.map(forward_visit, blocks)
    return (attended.reshape(length, local), logsum)


def backward_image(items):
    query, keys, values, attended, grad_out, logsum, valid = items
    length, local = query.shape
    heads = local // HD
    scale = HD ** (-0.5)
    block = min(512, length)
    count_blocks = length // block
    key_three = keys.reshape(length, heads, HD)
    value_three = values.reshape(length, heads, HD)
    blocks = (
        query.reshape(count_blocks, block, heads, HD),
        attended.reshape(count_blocks, block, heads, HD),
        grad_out.reshape(count_blocks, block, heads, HD),
        logsum,
    )
    zeros = jnp.zeros((length, heads, HD), jnp.float32)

    def backward_visit(carry, piece):
        query_block, out_block, grad_block, logsum_block = piece
        grad_keys, grad_values = carry
        scores = (
            jnp.einsum("qhd,khd->hqk", query_block, key_three, preferred_element_type=jnp.float32)
            * scale
        )
        scores = jnp.where(valid[None, None, :], scores, MASKED)
        chance = jnp.exp(scores - logsum_block[:, :, None])
        chance_low = chance.astype(jnp.bfloat16)
        grad_values = grad_values + jnp.einsum(
            "hqk,qhd->khd", chance_low, grad_block, preferred_element_type=jnp.float32
        )
        grad_chance = jnp.einsum(
            "qhd,khd->hqk", grad_block, value_three, preferred_element_type=jnp.float32
        )
        delta = jnp.sum(grad_block.astype(jnp.float32) * out_block.astype(jnp.float32), axis=-1).T
        grad_scores = (chance * (grad_chance - delta[:, :, None]) * scale).astype(jnp.bfloat16)
        grad_query = jnp.einsum(
            "hqk,khd->qhd", grad_scores, key_three, preferred_element_type=jnp.float32
        )
        grad_keys = grad_keys + jnp.einsum(
            "hqk,qhd->khd", grad_scores, query_block, preferred_element_type=jnp.float32
        )
        return ((grad_keys, grad_values), grad_query.astype(jnp.bfloat16))

    (grad_keys, grad_values), grad_query = lax.scan(backward_visit, (zeros, zeros), blocks)
    return (
        grad_query.reshape(length, local),
        grad_keys.astype(jnp.bfloat16).reshape(length, local),
        grad_values.astype(jnp.bfloat16).reshape(length, local),
    )


def shards(
    images,
    key_mask,
    attn_gain,
    attn_shift,
    query_weight,
    key_weight,
    value_weight,
    query_bias,
    value_bias,
    out_weight,
    out_bias,
    mlp_gain,
    mlp_shift,
    inner_weight,
    inner_bias,
    outer_weight,
    outer_bias,
    cotangent,
):
    gathered = (
        lax.all_gather(attn_gain, "fsdp", axis=0, tiled=True),
        lax.all_gather(attn_shift, "fsdp", axis=0, tiled=True),
        lax.all_gather(query_weight, "fsdp", axis=0, tiled=True),
        lax.all_gather(key_weight, "fsdp", axis=0, tiled=True),
        lax.all_gather(value_weight, "fsdp", axis=0, tiled=True),
        lax.all_gather(query_bias, "fsdp", axis=0, tiled=True),
        lax.all_gather(value_bias, "fsdp", axis=0, tiled=True),
        lax.all_gather(out_weight, "fsdp", axis=0, tiled=True),
        lax.all_gather(out_bias, "fsdp", axis=0, tiled=True),
        lax.all_gather(mlp_gain, "fsdp", axis=0, tiled=True),
        lax.all_gather(mlp_shift, "fsdp", axis=0, tiled=True),
        lax.all_gather(inner_weight, "fsdp", axis=0, tiled=True),
        lax.all_gather(inner_bias, "fsdp", axis=0, tiled=True),
        lax.all_gather(outer_weight, "fsdp", axis=0, tiled=True),
        lax.all_gather(outer_bias, "fsdp", axis=0, tiled=True),
    )
    (
        gain_attn,
        shift_attn,
        w_query,
        w_key,
        w_value,
        b_query,
        b_value,
        w_out,
        b_out,
        gain_mlp,
        shift_mlp,
        w_inner,
        b_inner,
        w_outer,
        b_outer,
    ) = gathered
    count, block_len, width = images.shape
    rows = count * block_len
    flat = images.reshape(rows, width).astype(jnp.float32)
    normed_one, factor_one = normalize(flat)
    hidden_one = (
        normed_one * gain_attn.astype(jnp.float32) + shift_attn.astype(jnp.float32)
    ).astype(jnp.bfloat16)
    query = (product(hidden_one, w_query) + b_query.astype(jnp.float32)).astype(jnp.bfloat16)
    keys = product(hidden_one, w_key).astype(jnp.bfloat16)
    values = (product(hidden_one, w_value) + b_value.astype(jnp.float32)).astype(jnp.bfloat16)
    query_heads, key_heads, value_heads = (
        lax.all_to_all(
            query.reshape(count, block_len, width), "seq", split_axis=2, concat_axis=1, tiled=True
        ),
        lax.all_to_all(
            keys.reshape(count, block_len, width), "seq", split_axis=2, concat_axis=1, tiled=True
        ),
        lax.all_to_all(
            values.reshape(count, block_len, width), "seq", split_axis=2, concat_axis=1, tiled=True
        ),
    )
    valid = key_mask > 0
    attended, logsum = lax.map(forward_image, (query_heads, key_heads, value_heads, valid))
    attended_tokens = lax.all_to_all(attended, "seq", split_axis=1, concat_axis=2, tiled=True)
    attended_flat = attended_tokens.reshape(rows, width)
    second = flat + product(attended_flat, w_out) + b_out.astype(jnp.float32)
    normed_two, factor_two = normalize(second)
    hidden_two = (normed_two * gain_mlp.astype(jnp.float32) + shift_mlp.astype(jnp.float32)).astype(
        jnp.bfloat16
    )
    inner = product(hidden_two, w_inner) + b_inner.astype(jnp.float32)
    active = gelu_tanh(inner).astype(jnp.bfloat16)
    layer_out = second + product(active, w_outer) + b_outer.astype(jnp.float32)
    unpacked = (
        lax.all_gather(attn_gain, "fsdp", axis=0, tiled=True),
        lax.all_gather(attn_shift, "fsdp", axis=0, tiled=True),
        lax.all_gather(query_weight, "fsdp", axis=0, tiled=True),
        lax.all_gather(key_weight, "fsdp", axis=0, tiled=True),
        lax.all_gather(value_weight, "fsdp", axis=0, tiled=True),
        lax.all_gather(query_bias, "fsdp", axis=0, tiled=True),
        lax.all_gather(value_bias, "fsdp", axis=0, tiled=True),
        lax.all_gather(out_weight, "fsdp", axis=0, tiled=True),
        lax.all_gather(out_bias, "fsdp", axis=0, tiled=True),
        lax.all_gather(mlp_gain, "fsdp", axis=0, tiled=True),
        lax.all_gather(mlp_shift, "fsdp", axis=0, tiled=True),
        lax.all_gather(inner_weight, "fsdp", axis=0, tiled=True),
        lax.all_gather(inner_bias, "fsdp", axis=0, tiled=True),
        lax.all_gather(outer_weight, "fsdp", axis=0, tiled=True),
        lax.all_gather(outer_bias, "fsdp", axis=0, tiled=True),
    )
    (
        gain_attn,
        shift_attn,
        w_query,
        w_key,
        w_value,
        b_query,
        b_value,
        w_out,
        b_out,
        gain_mlp,
        shift_mlp,
        w_inner,
        b_inner,
        w_outer,
        b_outer,
    ) = unpacked
    upstream = cotangent.reshape(rows, width)
    grad_active = product_back(upstream, w_outer)
    grad_inner = jax.vjp(gelu_tanh, inner)[1](grad_active)[0]
    grad_inner_low = grad_inner.astype(jnp.bfloat16)
    grad_hidden_two = product_back(grad_inner_low, w_inner)
    grad_second = upstream.astype(jnp.float32) + norm_back(
        grad_hidden_two * gain_mlp.astype(jnp.float32), normed_two, factor_two
    )
    mlp_terms = (
        jnp.sum(grad_hidden_two * normed_two, axis=0),
        jnp.sum(grad_hidden_two, axis=0),
        product_rows(hidden_two, grad_inner_low),
        jnp.sum(grad_inner, axis=0),
        product_rows(active, upstream),
        jnp.sum(upstream.astype(jnp.float32), axis=0),
    )
    grad_second_low = grad_second.astype(jnp.bfloat16)
    grad_attended = product_back(grad_second_low, w_out).astype(jnp.bfloat16)
    grad_heads = lax.all_to_all(
        grad_attended.reshape(count, block_len, width),
        "seq",
        split_axis=2,
        concat_axis=1,
        tiled=True,
    )
    grad_query_heads, grad_key_heads, grad_value_heads = lax.map(
        backward_image, (query_heads, key_heads, value_heads, attended, grad_heads, logsum, valid)
    )
    grad_query, grad_keys, grad_values = (
        lax.all_to_all(grad_query_heads, "seq", split_axis=1, concat_axis=2, tiled=True),
        lax.all_to_all(grad_key_heads, "seq", split_axis=1, concat_axis=2, tiled=True),
        lax.all_to_all(grad_value_heads, "seq", split_axis=1, concat_axis=2, tiled=True),
    )
    grad_query = grad_query.reshape(rows, width)
    grad_keys = grad_keys.reshape(rows, width)
    grad_values = grad_values.reshape(rows, width)
    grad_hidden_one = (
        product_back(grad_query, w_query)
        + product_back(grad_keys, w_key)
        + product_back(grad_values, w_value)
    )
    images_grad = grad_second + norm_back(
        grad_hidden_one * gain_attn.astype(jnp.float32), normed_one, factor_one
    )
    attn_terms = (
        jnp.sum(grad_hidden_one * normed_one, axis=0),
        jnp.sum(grad_hidden_one, axis=0),
        product_rows(hidden_one, grad_query),
        product_rows(hidden_one, grad_keys),
        product_rows(hidden_one, grad_values),
        jnp.sum(grad_query.astype(jnp.float32), axis=0),
        jnp.sum(grad_values.astype(jnp.float32), axis=0),
        product_rows(attended_flat, grad_second_low),
        jnp.sum(grad_second, axis=0),
    )
    shard_grads = (
        lax.psum_scatter(attn_terms[0], "fsdp", scatter_dimension=0, tiled=True),
        lax.psum_scatter(attn_terms[1], "fsdp", scatter_dimension=0, tiled=True),
        lax.psum_scatter(attn_terms[2], "fsdp", scatter_dimension=0, tiled=True),
        lax.psum_scatter(attn_terms[3], "fsdp", scatter_dimension=0, tiled=True),
        lax.psum_scatter(attn_terms[4], "fsdp", scatter_dimension=0, tiled=True),
        lax.psum_scatter(attn_terms[5], "fsdp", scatter_dimension=0, tiled=True),
        lax.psum_scatter(attn_terms[6], "fsdp", scatter_dimension=0, tiled=True),
        lax.psum_scatter(attn_terms[7], "fsdp", scatter_dimension=0, tiled=True),
        lax.psum_scatter(attn_terms[8], "fsdp", scatter_dimension=0, tiled=True),
        lax.psum_scatter(mlp_terms[0], "fsdp", scatter_dimension=0, tiled=True),
        lax.psum_scatter(mlp_terms[1], "fsdp", scatter_dimension=0, tiled=True),
        lax.psum_scatter(mlp_terms[2], "fsdp", scatter_dimension=0, tiled=True),
        lax.psum_scatter(mlp_terms[3], "fsdp", scatter_dimension=0, tiled=True),
        lax.psum_scatter(mlp_terms[4], "fsdp", scatter_dimension=0, tiled=True),
        lax.psum_scatter(mlp_terms[5], "fsdp", scatter_dimension=0, tiled=True),
    )
    summed = lax.psum(
        (
            shard_grads[0],
            shard_grads[1],
            shard_grads[2],
            shard_grads[3],
            shard_grads[4],
            shard_grads[5],
            shard_grads[6],
            shard_grads[7],
            shard_grads[8],
            shard_grads[9],
            shard_grads[10],
            shard_grads[11],
            shard_grads[12],
            shard_grads[13],
            shard_grads[14],
        ),
        "seq",
    )
    return (
        layer_out.reshape(count, block_len, width),
        images_grad.reshape(count, block_len, width),
        summed[0],
        summed[1],
        summed[2],
        summed[3],
        summed[4],
        summed[5],
        summed[6],
        summed[7],
        summed[8],
        summed[9],
        summed[10],
        summed[11],
        summed[12],
        summed[13],
        summed[14],
    )


def solution(mesh):
    placed = (
        P("fsdp", "seq", None),
        P("fsdp", None),
        P("fsdp"),
        P("fsdp"),
        P("fsdp", None),
        P("fsdp", None),
        P("fsdp", None),
        P("fsdp"),
        P("fsdp"),
        P("fsdp", None),
        P("fsdp"),
        P("fsdp"),
        P("fsdp"),
        P("fsdp", None),
        P("fsdp"),
        P("fsdp", None),
        P("fsdp"),
        P("fsdp", "seq", None),
    )
    return jax.shard_map(
        shards,
        mesh=mesh,
        in_specs=placed,
        out_specs=(
            P("fsdp", "seq", None),
            P("fsdp", "seq", None),
            P("fsdp"),
            P("fsdp"),
            P("fsdp", None),
            P("fsdp", None),
            P("fsdp", None),
            P("fsdp"),
            P("fsdp"),
            P("fsdp", None),
            P("fsdp"),
            P("fsdp"),
            P("fsdp"),
            P("fsdp", None),
            P("fsdp"),
            P("fsdp", None),
            P("fsdp"),
        ),
        check_vma=False,
    )
```

profile of v0, /device:TPU:0, one launch (start us, length us, event | category | flops | bytes accessed | tf_op | source)
XLA Modules:
  0.0 1205.4 jit_solution(2965813202933017199)
XLA Ops:
  15.5 33.4 %all-reduce.23 = (bf16[1152]{0:T(1024)(128)(2,1)S(1)}, bf16[1152]{0:T(1024)(128)(2,1)S(1)}, bf16[1152]{0:T(1024)(128)(2,1)S(1)}, bf16[1152]{0:T(1024)(128)(2,1)S...) all-reduce(bf16[1152]{0:T(1024)(128)(2,1)S(1)} %dynamic-update-slic, ...), channel_id=1, replica_groups=mesh['seq'=4,'fsdp'=8] {'fsdp'}, use_global_device_ids=true, to_apply=%add.1 | all-reduce | flops 13520 | bytes 54080
  51.2 3.5 fusion.25
  54.6 2.0 copy.63
  56.6 3.6 all-to-all-start
  60.2 22.2 %all-gather.12.cloned.1.call-done = bf16[1152,1152]{1,0:T(8,128)(2,1)} async-done(((bf16[144,1152]{1,0:T(8,128)(2,1)}), bf16[1152,1152]{1,0:T(8,128)(2,1)}) %all-gather.12.cloned.1.call-update) | async-done | bytes 2654224 | tf_op jit(solution)/shard_map/all_gather | solution.py:146
  82.4 4.1 convolution_convert_fusion.3
  86.4 3.2 copy.69
  89.7 3.6 all-to-all-start.2
  93.3 23.8 %all-gather.10.cloned.1.call-done = bf16[1152,1152]{1,0:T(8,128)(2,1)} async-done(((bf16[144,1152]{1,0:T(8,128)(2,1)}), bf16[1152,1152]{1,0:T(8,128)(2,1)}) %all-gather.10.cloned.1.call-update) | async-done | bytes 2654224 | tf_op jit(solution)/shard_map/all_gather | solution.py:145
  117.2 4.4 fusion.26
  121.5 3.2 copy.66
  124.8 4.5 all-to-all-start.1
  130.6 14.4 %all-to-all-done.1 = bf16[3,128,1152]{1,0,2:T(4,128)(2,1)} async-done(((bf16[3,128,1152]{1,0,2:T(4,128)(2,1)}), bf16[3,128,1152]{1,0,2:T(4,128)(2,1)}, u32[]{:S(2)}, u32[]{:S(2)}) %all-to-all-start.1) | async-done | bytes 884768 | tf_op jit(solution)/shard_map/all_to_all | solution.py:187
  147.7 13.9 %while.10 = (s32[]{:T(128)}, bf16[3,512,288]{1,2,0:T(8,128)(2,1)}, f32[3,1,4,512]{3,2,1,0:T(4,128)}, bf16[3,512,288]{1,2,0:T(8,128)(2,1)S(1)}, pred[3,512]{1,0:T...) while((s32[]{:T(128)}, bf16[3,512,288]{1,2,0:T(8,128)(2,1)}, ...), condition=%wide.region_5.6_spmd, body=%wide.region_2.5_spmd.sunk | while | flops 313669632 | bytes 16190065 | solution.py:198
  161.5 3.5 copy.72
  165.0 4.3 all-to-all-start.3
  173.3 15.2 %all-to-all-done.3 = bf16[3,512,288]{2,0,1:T(4,128)(2,1)} async-done(((bf16[3,512,288]{2,0,1:T(4,128)(2,1)}), bf16[3,512,288]{2,0,1:T(4,128)(2,1)}, u32[]{:S(2)}, u32[]{:S(2)}) %all-to-all-start.3) | async-done | bytes 884768 | tf_op jit(solution)/shard_map/all_to_all | solution.py:199
  188.4 3.5 copy.99
  192.0 2.8 reshape.280
  194.8 3.6 fusion.42
  200.5 47.5 %all-gather.18.cloned.1.call-done = bf16[8,538,1152]{2,1,0:T(8,128)(2,1)} async-done(((bf16[1,538,1152]{2,1,0:T(8,128)(2,1)}), bf16[8,538,1152]{2,1,0:T(8,128)(2,1)}) %all-gather.18.cloned.1.call-update) | async-done | bytes 9916432 | tf_op jit(solution)/shard_map/all_gather | solution.py:156
  248.0 12.4 %reshape.318 = bf16[4304,1152]{1,0:T(8,128)(2,1)} reshape(bf16[8,538,1152]{2,1,0:T(8,128)(2,1)} %all-gather.18.cloned.1.call-done) | data formatting | bytes 19832832
  260.4 10.5 fusion.44
  270.9 72.6 %all-gather.16.cloned.1.call-done = bf16[1152,4304]{1,0:T(8,128)(2,1)} async-done(((bf16[144,4304]{1,0:T(8,128)(2,1)}), bf16[1152,4304]{1,0:T(8,128)(2,1)}) %all-gather.16.cloned.1.call-update) | async-done | bytes 9916432 | tf_op jit(solution)/shard_map/all_gather | solution.py:154
  343.5 20.9 %fusion.38 = (f32[4304]{0:T(1024)}, bf16[384,4304]{0,1:T(8,128)(2,1)S(1)}, f32[384,4304]{0,1:T(8,128)}) fusion(f32[384,4304]{0,1:T(8,128)} %fusion.44, f32[4304]{0:T(1024)} %convert_element_type.163, bf16[1152,4304]{1,0:T(8,128)(2,1)} %all-gather.16.cloned.1.call-done, f32[384,1152]{1,0:T(8,128)} %copy-done.1, f32[1152]{0:T(1024)} %convert_element_type.161, ...), kind=kOutput, calls=%fused_computation.108 | convolution fusion | flops 3846471424 | bytes 28259968 | tf_op jit(solution)/shard_map/dot_general | solution.py:12
  364.4 10.7 multiply_reduce_fusion
  377.7 4.0 fusion.32
  381.7 4.7 convolution_convert_fusion.2
  386.3 3.2 copy.74
  389.6 19.9 %all_to_all.132 = bf16[3,128,1152]{1,0,2:T(4,128)(2,1)S(1)} all-to-all(bf16[3,128,1152]{1,0,2:T(4,128)(2,1)} %copy.74), channel_id=1, replica_groups=mesh['seq'=4,'fsdp'=8] {'seq'}, dimensions={2} | all-to-all | bytes 1769472 | tf_op jit(solution)/shard_map/all_to_all | solution.py:261
  413.7 27.9 %while.27 = (s32[]{:T(128)}, bf16[3,512,288]{1,2,0:T(8,128)(2,1)}, bf16[3,512,288]{1,2,0:T(8,128)(2,1)}, bf16[3,512,288]{1,2,0:T(8,128)(2,1)}, bf16[3,512,288]{1...) while((s32[]{:T(128)}, bf16[3,512,288]{1,2,0:T(8,128)(2,1)}, ...), condition=%wide.region_12.13_spmd, body=%wide.region_10.12_spmd.sunk | while | flops 767539200 | bytes 27183264 | solution.py:268
  417.4 1.7 multiply_convert_fusion.5
  426.7 1.7 multiply_convert_fusion.5
  436.0 1.8 multiply_convert_fusion.5
  441.6 3.4 copy.77
  445.0 3.6 all-to-all-start.5
  449.0 18.1 %all-to-all-done.5 = bf16[3,512,288]{2,0,1:T(4,128)(2,1)S(1)} async-done(((bf16[3,512,288]{2,0,1:T(4,128)(2,1)}), bf16[3,512,288]{2,0,1:T(4,128)(2,1)S(1)}, u32[]{:S(2)}, u32[]{:S(2)}) %all-to-all-start.5) | async-done | bytes 884768 | tf_op jit(solution)/shard_map/all_to_all | solution.py:272
  467.2 2.8 convert_reduce_fusion.1
  470.0 2.1 reshape.284
  472.1 4.0 fusion.46
  476.1 2.8 copy.79
  478.9 21.9 %all_to_all.133 = bf16[3,512,288]{2,0,1:T(4,128)(2,1)S(1)} all-to-all(bf16[3,512,288]{2,0,1:T(4,128)(2,1)S(1)} %copy.79), channel_id=1, replica_groups=mesh['seq'=4,'fsdp'=8] {'seq'}, dimensions={1} | all-to-all | bytes 1769472 | tf_op jit(solution)/shard_map/all_to_all | solution.py:273
  503.7 5.2 fusion.47
  509.0 2.8 copy.81
  511.8 20.5 %all_to_all.134 = bf16[3,512,288]{2,0,1:T(4,128)(2,1)S(1)} all-to-all(bf16[3,512,288]{2,0,1:T(4,128)(2,1)S(1)} %copy.81), channel_id=1, replica_groups=mesh['seq'=4,'fsdp'=8] {'seq'}, dimensions={1} | all-to-all | bytes 1769472 | tf_op jit(solution)/shard_map/all_to_all | solution.py:274
  532.3 1.8 convert_reduce_fusion
  534.1 1.7 reshape.286
  535.8 5.2 fusion.48
  542.5 11.6 fusion.28
  555.3 15.7 %fusion.37 = f32[4304,1152]{1,0:T(8,128)} fusion(bf16[384,1152]{1,0:T(8,128)(2,1)S(1)} %bitcast.215, f32[384,4304]{0,1:T(8,128)} %get-tuple-element.275), kind=kOutput, calls=%fused_computation.107 | convolution fusion | flops 3822778368 | bytes 27328512 | tf_op jit(solution)/shard_map/dot_general | solution.py:16
  571.0 387.5 %fusion = f32[544,1152]{1,0:T(8,128)} fusion(f32[4304,1152]{1,0:T(8,128)} %fusion.37), kind=kCustom, calls=%all-reduce-scatter | all-reduce-scatter fusion | flops 5013505 | bytes 22340096
  960.1 2.0 collective-permute-start
  962.8 9.9 concatenate
  972.7 3.4 constant_dynamic-slice_fusion.8
  976.1 45.6 %reduce-scatter.16.cloned.1.call-done = f32[144,4304]{1,0:T(8,128)} async-done(((f32[1152,4304]{1,0:T(8,128)}), f32[144,4304]{1,0:T(8,128)}) %reduce-scatter.16.cloned.1.call-update) | async-done | bytes 2479120 | tf_op jit(solution)/shard_map/reduce_scatter | solution.py:310
  1023.9 11.6 fusion.24
  1037.6 3.4 fusion.45
  1043.6 2.9 multiply_reduce_fusion.1
  1046.5 29.1 %all-reduce.20 = (f32[1152]{0:T(1024)S(1)}, f32[1152]{0:T(1024)S(1)}, f32[1152]{0:T(1024)S(1)}, f32[1152]{0:T(1024)S(1)}, f32[1152]{0:T(1024)S(1)}, /*index=5*/f...) all-reduce(f32[1152]{0:T(1024)S(1)} %get-tuple-element.175, ...), channel_id=2, replica_groups=mesh['seq'=4,'fsdp'=8] {'fsdp'}, use_global_device_ids=true, to_apply=%region_16.17.clone | all-reduce | flops 13520 | bytes 108160
  1076.2 17.0 %all-reduce.21 = (f32[144]{0:T(256)}, f32[144]{0:T(256)}, f32[144]{0:T(256)}, f32[144]{0:T(256)}, f32[144]{0:T(256)}, /*index=5*/f32[144]{0:T(256)}, f32[144]{0:T(256)}, f32[538]{0:T(1024)}, f32[144]{0:T(256)}) all-reduce(f32[144]{0:T(256)S(1)} %dynamic-slice.10, ...), channel_id=1, replica_groups=mesh['seq'=4,'fsdp'=8] {'seq'}, use_global_device_ids=true, to_apply=%region_17.18 | all-reduce | flops 1690 | bytes 13520 | tf_op jit(solution)/shard_map/psum | solution.py:315
  1093.2 3.3 multiply_add_fusion
  1096.5 91.7 %all-reduce.26.cloned.1.call-done = (f32[144,1152]{1,0:T(8,128)}, f32[144,1152]{1,0:T(8,128)}, f32[144,1152]{1,0:T(8,128)}, f32[144,1152]{1,0:T(8,128)}, f32[144,4304]{1,0:T(8,128)}, /*index=5*/f32[538,1152]{1,0:T(8,128)}) async-done(((f32[144,1152]{1,0:T(8,128)}, f32[144,1152]{1,0:T(8,128)}, f32[144,1152]{1,0:T(8,128)}, f32[144,1152]{1,0:T(8,128)}, f32[144,4304]{1,0:T(8,128)}, ...) | async-done | bytes 7612432 | tf_op jit(solution)/shard_map/psum | solution.py:315
  1188.2 2.1 copy.145
  1190.4 2.0 copy.146
  (282 shorter events, 81.7 us)
Async XLA Ops:
  7.2 4.1 copy-start.41
  7.2 6.0 copy-start.46
  7.2 6.2 copy-start.47
  7.2 6.5 copy-start.48
  7.2 6.7 copy-start.49
  7.2 7.0 copy-start.50
  7.3 7.2 copy-start.51
  7.3 7.5 copy-start.52
  7.3 7.7 copy-start.53
  7.3 7.9 copy-start.43
  7.3 41.6 %copy-start = (bf16[3,128,1152]{2,1,0:T(8,128)(2,1)S(1)}, bf16[3,128,1152]{2,1,0:T(8,128)(2,1)}, u32[]{:S(2)}) copy-start(bf16[3,128,1152]{2,1,0:T(8,128)(2,1)} %param.22) | copy-start | bytes 2654212
  7.3 43.8 %all-gather.8.cloned.1.call-start = ((), (), s32[]{:S(2)}) async-start(), calls=%async_computation.13 | async-start | bytes 2985984 | tf_op jit(solution)/shard_map/all_gather | solution.py:147
  8.0 74.3 %all-gather.12.cloned.1.call-start = ((), (), s32[]{:S(2)}) async-start(), calls=%async_computation.15 | async-start | bytes 2985984 | tf_op jit(solution)/shard_map/all_gather | solution.py:146
  8.8 108.4 %all-gather.10.cloned.1.call-start = ((), (), s32[]{:S(2)}) async-start(), calls=%async_computation.14 | async-start | bytes 2985984 | tf_op jit(solution)/shard_map/all_gather | solution.py:145
  9.5 185.3 %all-gather.14.cloned.1.call-start = ((), (), s32[]{:S(2)}) async-start(), calls=%async_computation.16 | async-start | bytes 2985984 | tf_op jit(solution)/shard_map/all_gather | solution.py:150
  10.1 237.9 %all-gather.18.cloned.1.call-start = ((), (), s32[]{:S(2)}) async-start(), calls=%async_computation.23 | async-start | bytes 11280384 | tf_op jit(solution)/shard_map/all_gather | solution.py:156
  10.7 332.8 %all-gather.16.cloned.1.call-start = ((), (), s32[]{:S(2)}) async-start(), calls=%async_computation.17 | async-start | bytes 11280384 | tf_op jit(solution)/shard_map/all_gather | solution.py:154
  51.1 31.3 %copy-start.17 = (bf16[384,1152]{1,0:T(8,128)(2,1)}, bf16[384,1152]{1,0:T(8,128)(2,1)S(1)}, u32[]{:S(2)}) copy-start(bf16[384,1152]{1,0:T(8,128)(2,1)S(1)} %add_convert_fusion.2) | copy-start | bytes 2654212
  56.6 33.1 %all-to-all-start = ((bf16[3,128,1152]{1,0,2:T(4,128)(2,1)}), bf16[3,128,1152]{1,0,2:T(4,128)(2,1)S(1)}, u32[]{:S(2)}, u32[]{:S(2)}) async-start(bf16[3,128,1152]{1,0,2:T(4,128)(2,1)} %copy.63), calls=%async_computation | async-start | bytes 2359296 | tf_op jit(solution)/shard_map/all_to_all | solution.py:193
  89.7 35.1 %all-to-all-start.2 = ((bf16[3,128,1152]{1,0,2:T(4,128)(2,1)}), bf16[3,128,1152]{1,0,2:T(4,128)(2,1)S(1)}, u32[]{:S(2)}, u32[]{:S(2)}) async-start(bf16[3,128,1152]{1,0,2:T(4,128)(2,1)} %copy.69), calls=%async_computation.2 | async-start | bytes 2359296 | tf_op jit(solution)/shard_map/all_to_all | solution.py:190
  121.5 7.8 copy-start.38
  124.8 20.2 %all-to-all-start.1 = ((bf16[3,128,1152]{1,0,2:T(4,128)(2,1)}), bf16[3,128,1152]{1,0,2:T(4,128)(2,1)}, u32[]{:S(2)}, u32[]{:S(2)}) async-start(bf16[3,128,1152]{1,0,2:T(4,128)(2,1)} %copy.66), calls=%async_computation.1 | async-start | bytes 2359296 | tf_op jit(solution)/shard_map/all_to_all | solution.py:187
  145.0 1.5 copy-start.13
  165.0 23.4 %all-to-all-start.3 = ((bf16[3,512,288]{2,0,1:T(4,128)(2,1)}), bf16[3,512,288]{2,0,1:T(4,128)(2,1)}, u32[]{:S(2)}, u32[]{:S(2)}) async-start(bf16[3,512,288]{2,0,1:T(4,128)(2,1)} %copy.72), calls=%async_computation.3 | async-start | bytes 3145728 | tf_op jit(solution)/shard_map/all_to_all | solution.py:199
  169.3 806.7 %reduce-scatter.14.cloned.1.call-start = ((), (), s32[]{:S(2)}) async-start(), calls=%async_computation.21 | async-start | bytes 5971968 | tf_op jit(solution)/shard_map/reduce_scatter | solution.py:306
  198.4 1.2 copy-start.1
  343.5 20.9 %copy-start.2 = (f32[384,1152]{1,0:T(8,128)S(1)}, f32[384,1152]{1,0:T(8,128)}, u32[]{:S(2)}) copy-start(f32[384,1152]{1,0:T(8,128)} %copy-done.1) | copy-start | bytes 5308420
  343.5 20.9 %copy-start.26 = (f32[384]{0:T(512)S(1)}, f32[384]{0:T(512)}, u32[]{:S(2)}) copy-start(f32[384]{0:T(512)} %add_rsqrt_fusion) | copy-start | bytes 4612
  364.4 10.7 copy-start.14
  364.4 10.7 copy-start.6
  375.1 2.5 copy-start.8
  441.6 7.0 copy-start.21
  441.6 7.0 copy-start.25
  441.6 7.0 copy-start.36
  441.6 7.0 copy-start.37
  445.0 22.2 %all-to-all-start.5 = ((bf16[3,512,288]{2,0,1:T(4,128)(2,1)}), bf16[3,512,288]{2,0,1:T(4,128)(2,1)S(1)}, u32[]{:S(2)}, u32[]{:S(2)}) async-start(bf16[3,512,288]{2,0,1:T(4,128)(2,1)} %copy.77), calls=%async_computation.5 | async-start | bytes 3145728 | tf_op jit(solution)/shard_map/all_to_all | solution.py:272
  448.5 527.5 %reduce-scatter.8.cloned.1.call-start = ((), (), s32[]{:S(2)}) async-start(), calls=%async_computation.18 | async-start | bytes 5971968 | tf_op jit(solution)/shard_map/reduce_scatter | solution.py:301
  472.1 4.0 copy-start.9
  476.1 500.0 %reduce-scatter.10.cloned.1.call-start = ((), (), s32[]{:S(2)}) async-start(), calls=%async_computation.19 | async-start | bytes 5971968 | tf_op jit(solution)/shard_map/reduce_scatter | solution.py:302
  508.9 467.2 %reduce-scatter.12.cloned.1.call-start = ((), (), s32[]{:S(2)}) async-start(), calls=%async_computation.20 | async-start | bytes 5971968 | tf_op jit(solution)/shard_map/reduce_scatter | solution.py:303
  541.0 1.5 copy-start.3
  541.0 1.5 copy-start.23
  541.0 1.5 copy-start.27
  541.0 480.7 %reduce-scatter.16.cloned.1.call-start = ((), (), s32[]{:S(2)}) async-start(), calls=%async_computation.22 | async-start | bytes 22560768 | tf_op jit(solution)/shard_map/reduce_scatter | solution.py:310
  554.1 634.1 %all-reduce.26.cloned.1.call-start = ((), (), s32[]{:S(2)}) async-start(), calls=%async_computation.24 | async-start | bytes 15335424 | tf_op jit(solution)/shard_map/psum | solution.py:315
  960.1 2.7 collective-permute-start
  1023.9 13.8 %copy-start.10 = (bf16[384,1152]{1,0:T(8,128)(2,1)S(1)}, bf16[384,1152]{1,0:T(8,128)(2,1)}, u32[]{:S(2)}) copy-start(bf16[384,1152]{1,0:T(8,128)(2,1)} %copy-done.9) | copy-start | bytes 2654212
  1037.6 3.4 copy-start.11
  1037.6 3.4 copy-start.45
  1041.0 1.5 copy-start.12
  1041.0 1.5 copy-start.22
  1041.0 1.5 copy-start.32
  1041.0 1.5 copy-start.34
  1041.1 2.5 copy-start.44
  1043.5 2.9 copy-start.28
  1043.5 3.0 copy-start.29
  1043.5 3.0 copy-start.30
  1043.5 3.0 copy-start.39
  1043.5 3.0 copy-start.40
  1043.5 49.7 %copy-start.5 = (f32[384,1152]{1,0:T(8,128)S(1)}, f32[384,1152]{1,0:T(8,128)}, u32[]{:S(2)}) copy-start(f32[384,1152]{1,0:T(8,128)} %copy-done.4) | copy-start | bytes 5308420
  1188.2 4.1 copy-start.19
  1188.2 4.9 copy-start.18
  1188.2 5.8 copy-start.16
  1194.0 2.6 copy-start.15
  (8 other events, 8.0 us)
Sparse Core Ops, SparseCore 0:
  9.8 37.7 all-gather.7
  49.1 33.1 all-gather.11
  84.0 33.0 all-gather.9
  118.6 33.0 all-gather.13
  153.3 94.6 all-gather.17
  249.5 93.9 all-gather.15
  381.8 58.8 reduce-scatter.13
  476.2 57.8 reduce-scatter.7
  536.4 74.3 reduce-scatter.9
  612.9 111.5 reduce-scatter.11
  726.9 294.8 reduce-scatter.15
  1026.6 161.5 all-reduce.25
where the time goes:
time: 1210 us
  blocking collectives  529 us (44%)
  waiting for transfers between devices  355 us (29%)
  matrix products  148 us (12%)
  local copies, waits for them, and re-layouts  111 us (9%)
  starting transfers between devices  22.1 us (2%)
  other arithmetic  21 us (2%)
  between operations  18.5 us (2%)
    unnamed x3, blocking collectives  450 us
    psum x1, waiting for transfers between devices, shards(): lax.psum((shard_grads[0], shard_grads[1], shard_grads[2], shard_grads[3],...  91.7 us
    all_gather x1, waiting for transfers between devices, shards(): lax.all_gather(inner_weight, 'fsdp', axis=0, tiled=True)  72.6 us
    dot_general x6, matrix products, product(): return jnp.dot(left, right, preferred_element_type=jnp.float32)  48 us
    unnamed x146, local copies, waits for them, and re-layouts  47.9 us
    all_gather x1, waiting for transfers between devices, shards(): lax.all_gather(outer_weight, 'fsdp', axis=0, tiled=True)  47.5 us
    dot_general x6, matrix products, product_rows(): lax.dot_general(left, right, (((0,), (0,)), ((), ())), preferred_element_...  45.7 us
    reduce_scatter x1, waiting for transfers between devices, shards(): lax.psum_scatter(mlp_terms[2], 'fsdp', scatter_dimension=0, tiled=True)  45.6 us
  transfers between devices with their start and end apart: 18, of which 10 were waited for; matrix products, arithmetic and copies ran while one was open for 51% of the time, Pallas kernels for 0%

commit v1 on v0

--- a/solution.py
+++ b/solution.py
@@ -6,6 +6,19 @@
 HD = 72
 EPSILON = 1e-06
 MASKED = -1e30
+
+
+def gather_around(x, axis, dim):
+    ways = lax.axis_size(axis)
+    up = [(d, (d + 1) % ways) for d in range(ways)]
+    down = [(d, (d - 1) % ways) for d in range(ways)]
+    earlier, later = ([x], [x])
+    for _ in range(ways // 2):
+        earlier.append(lax.ppermute(earlier[-1], axis, up))
+    for _ in range((ways - 1) // 2):
+        later.append(lax.ppermute(later[-1], axis, down))
+    line = jnp.concatenate([*earlier[::-1], *later[1:]], axis=dim)
+    return jnp.roll(line, (lax.axis_index(axis) - ways // 2) * x.shape[dim], axis=dim)
 
 
 def product(left, right):
@@ -151,7 +164,7 @@
         lax.all_gather(out_bias, "fsdp", axis=0, tiled=True),
         lax.all_gather(mlp_gain, "fsdp", axis=0, tiled=True),
         lax.all_gather(mlp_shift, "fsdp", axis=0, tiled=True),
-        lax.all_gather(inner_weight, "fsdp", axis=0, tiled=True),
+        gather_around(inner_weight, "fsdp", 0),
         lax.all_gather(inner_bias, "fsdp", axis=0, tiled=True),
         lax.all_gather(outer_weight, "fsdp", axis=0, tiled=True),
         lax.all_gather(outer_bias, "fsdp", axis=0, tiled=True),

time: 1210 us -> 1240 us (1.025)
  waiting for transfers between devices: 355 us -> 284 us
  blocking collectives: 529 us -> 576 us
  local copies, waits for them, and re-layouts: 111 us -> 143 us
  starting transfers between devices: 22.1 us -> 47.9 us
    ppermute x0 -> x7, waiting for transfers between devices: none -> 68.8 us  [the longest x4 68.7 us: gather_around(): earlier.append(lax.ppermute(earlier[-1], axis, up))]
    all_gather x1, waiting for transfers between devices: 47.5 us -> 0.01 us  [shards(): lax.all_gather(outer_weight, 'fsdp', axis=0, tiled=True)]
    unnamed x3, blocking collectives: 450 us -> 496 us
    all_gather x1, waiting for transfers between devices: 72.6 us -> 32.9 us  [shards(): lax.all_gather(inner_weight, 'fsdp', axis=0, tiled=True)]
    unnamed x146 -> x183, local copies, waits for them, and re-layouts: 47.9 us -> 74 us
    ppermute x0 -> x7, starting transfers between devices: none -> 24.1 us  [the longest x4 15 us: gather_around(): earlier.append(lax.ppermute(earlier[-1], axis, up))]
    all_gather x1, waiting for transfers between devices: 23.8 us -> 0.01 us  [shards(): lax.all_gather(query_weight, 'fsdp', axis=0, tiled=True)]
    all_gather x1, waiting for transfers between devices: 22.2 us -> 0.02 us  [shards(): lax.all_gather(key_weight, 'fsdp', axis=0, tiled=True)]
  transfers between devices with their start and end apart: 18 -> 25, of which waited for: 10 -> 12; matrix products, arithmetic and copies ran while one was open for 51% -> 54% of each run, Pallas kernels for 0% -> 0%
where the time goes in v1:
time: 1240 us; the launch traced here: 1230 us
  blocking collectives  576 us (46%)
  waiting for transfers between devices  284 us (23%)
  matrix products  145 us (12%)
  local copies, waits for them, and re-layouts  143 us (12%)
  starting transfers between devices  47.9 us (4%)
  other arithmetic  19.9 us (2%)
  between operations  18.6 us (2%)
    unnamed x3, blocking collectives  496 us
    psum x1, waiting for transfers between devices, shards(): lax.psum((shard_grads[0], shard_grads[1], shard_grads[2], shard_grads[3],...  92.1 us
    unnamed x183, local copies, waits for them, and re-layouts  74 us
    ppermute x4, waiting for transfers between devices, gather_around(): earlier.append(lax.ppermute(earlier[-1], axis, up))  68.7 us
    reduce_scatter x1, waiting for transfers between devices, shards(): lax.psum_scatter(mlp_terms[2], 'fsdp', scatter_dimension=0, tiled=True)  45.8 us
    dot_general x6, matrix products, product(): return jnp.dot(left, right, preferred_element_type=jnp.float32)  45.7 us
    dot_general x6, matrix products, product_rows(): lax.dot_general(left, right, (((0,), (0,)), ((), ())), preferred_element_...  45.6 us
    all_gather x1, waiting for transfers between devices, shards(): lax.all_gather(inner_weight, 'fsdp', axis=0, tiled=True)  32.9 us
  transfers between devices with their start and end apart: 25, of which 12 were waited for; matrix products, arithmetic and copies ran while one was open for 54% of the time, Pallas kernels for 0%

profile of v1, /device:TPU:0, one launch (start us, length us, event | category | flops | bytes accessed | tf_op | source)
XLA Modules:
  0.0 1234.3 jit_solution(7012619822541522138)
XLA Ops:
  11.3 30.1 %collective-permute-done = bf16[144,4304]{1,0:T(8,128)(2,1)S(1)} collective-permute-done((bf16[144,4304]{1,0:T(8,128)(2,1)}, bf16[144,4304]{1,0:T(8,128)(2,1)S(1)}, u32[]{:S(2)}, u32[]{:S(2)}) %collective-permute-start) | collective-permute-done | bytes 1239584 | tf_op jit(solution)/shard_map/ppermute | solution.py:17
  45.0 26.9 %collective-permute-done.1 = bf16[144,4304]{1,0:T(8,128)(2,1)} collective-permute-done((bf16[144,4304]{1,0:T(8,128)(2,1)S(1)}, bf16[144,4304]{1,0:T(8,128)(2,1)}, u32[]{:S(2)}, u32[]{:S(2)}) %collective-permute-start.1) | collective-permute-done | bytes 1239584 | tf_op jit(solution)/shard_map/ppermute | solution.py:17
  71.8 12.9 %collective-permute-start.2 = (bf16[144,4304]{1,0:T(8,128)(2,1)}, bf16[144,4304]{1,0:T(8,128)(2,1)}, u32[]{:S(2)}, u32[]{:S(2)}) collective-permute-start(bf16[144,4304]{1,0:T(8,128)(2,1)} %collective-permute-done.1), channel_id=1, source_target_pairs={{0,1},{1,2},{2,3},{3,4},{4,5},{5,6},{6,7},{7,0},{8,9},{9,10},{10,1... | collective-permute-start | bytes 3718664 | tf_op jit(solution)/shard_map/ppermute | solution.py:17
  85.0 3.7 collective-permute-start.5
  92.9 79.3 %all-reduce.23 = (bf16[1152]{0:T(1024)(128)(2,1)S(1)}, bf16[1152]{0:T(1024)(128)(2,1)S(1)}, bf16[1152]{0:T(1024)(128)(2,1)S(1)}, bf16[1152]{0:T(1024)(128)(2,1)S...) all-reduce(bf16[1152]{0:T(1024)(128)(2,1)S(1)} %dynamic-update-slic, ...), channel_id=1, replica_groups=mesh['seq'=4,'fsdp'=8] {'fsdp'}, use_global_device_ids=true, to_apply=%add.1 | all-reduce | flops 13520 | bytes 54080
  176.4 3.5 collective-permute-start.6
  179.9 4.4 fusion.31
  184.3 3.3 copy.66
  187.6 4.3 all-to-all-start.1
  192.0 4.1 convolution_convert_fusion.3
  196.1 3.2 copy.69
  199.3 4.1 fusion.30
  203.4 3.4 copy.63
  206.8 11.7 collective-permute-done.3
  218.5 2.5 constant_dynamic-update-slice_fusion.19
  221.0 2.6 constant_dynamic-update-slice_fusion.18
  223.6 2.5 constant_dynamic-update-slice_fusion.17
  230.8 2.5 constant_dynamic-update-slice_fusion.12
  235.7 2.5 constant_dynamic-update-slice_fusion.10
  238.2 4.4 all-to-all-start
  246.1 11.3 all-to-all-done
  257.5 4.7 all-to-all-start.2
  268.4 4.0 all-to-all-done.2
  275.1 13.8 %while.10 = (s32[]{:T(128)}, bf16[3,512,288]{1,2,0:T(8,128)(2,1)}, f32[3,1,4,512]{3,2,1,0:T(4,128)}, bf16[3,512,288]{1,2,0:T(8,128)(2,1)S(1)}, pred[3,512]{1,0:T...) while((s32[]{:T(128)}, bf16[3,512,288]{1,2,0:T(8,128)(2,1)}, ...), condition=%wide.region_5.6_spmd, body=%wide.region_2.5_spmd.sunk | while | flops 313669632 | bytes 16191073 | solution.py:211
  288.9 3.4 copy.72
  292.3 4.4 all-to-all-start.3
  301.5 7.4 all-to-all-done.3
  308.9 3.5 copy.99
  312.5 2.8 reshape.280
  315.3 3.5 fusion.48
  320.9 11.8 reshape.318
  332.8 9.1 fusion.50
  341.9 18.0 %fusion.44 = (f32[4304]{0:T(1024)}, bf16[384,4304]{0,1:T(8,128)(2,1)}, f32[384,4304]{0,1:T(8,128)}) fusion(f32[384,4304]{0,1:T(8,128)S(1)} %fusion.50, f32[4304]{0:T(1024)S(1)} %copy-done.40, bf16[2304,4304]{1,0:T(8,128)(2,1)} %constant_dynamic-update-slice_fusion.4, s32[]{:T(128)S(6)} %select_n.23, f32[384,1152]{1,0:T(8,128)S(1)} %copy-done.2, ...), kind=kOutput, calls=%fused_computation.127 | convolution fusion | flops 3846471424 | bytes 28370564 | tf_op jit(solution)/shard_map/dot_general | solution.py:25
  359.9 32.9 %all-gather.16.cloned.1.call-done = bf16[1152,4304]{1,0:T(8,128)(2,1)} async-done(((bf16[144,4304]{1,0:T(8,128)(2,1)}), bf16[1152,4304]{1,0:T(8,128)(2,1)}) %all-gather.16.cloned.1.call-update) | async-done | bytes 9916432 | tf_op jit(solution)/shard_map/all_gather | solution.py:234
  392.8 11.1 multiply_reduce_fusion
  406.4 4.0 fusion.37
  410.4 4.7 convolution_convert_fusion.2
  415.1 3.2 copy.74
  418.3 20.1 %all_to_all.132 = bf16[3,128,1152]{1,0,2:T(4,128)(2,1)S(1)} all-to-all(bf16[3,128,1152]{1,0,2:T(4,128)(2,1)} %copy.74), channel_id=1, replica_groups=mesh['seq'=4,'fsdp'=8] {'seq'}, dimensions={2} | all-to-all | bytes 1769472 | tf_op jit(solution)/shard_map/all_to_all | solution.py:274
  442.6 27.9 %while.27 = (s32[]{:T(128)}, bf16[3,512,288]{1,2,0:T(8,128)(2,1)}, bf16[3,512,288]{1,2,0:T(8,128)(2,1)}, bf16[3,512,288]{1,2,0:T(8,128)(2,1)}, bf16[3,512,288]{1...) while((s32[]{:T(128)}, bf16[3,512,288]{1,2,0:T(8,128)(2,1)}, ...), condition=%wide.region_12.13_spmd, body=%wide.region_10.12_spmd.sunk | while | flops 767539200 | bytes 27184272 | solution.py:281
  470.5 3.4 copy.81
  473.9 3.6 all-to-all-start.7
  478.0 18.1 %all-to-all-done.7 = bf16[3,512,288]{2,0,1:T(4,128)(2,1)S(1)} async-done(((bf16[3,512,288]{2,0,1:T(4,128)(2,1)}), bf16[3,512,288]{2,0,1:T(4,128)(2,1)S(1)}, u32[]{:S(2)}, u32[]{:S(2)}) %all-to-all-start.7) | async-done | bytes 884768 | tf_op jit(solution)/shard_map/all_to_all | solution.py:287
  496.1 2.8 convert_reduce_fusion
  501.0 4.0 fusion.54
  505.1 2.8 copy.77
  507.9 21.9 %all_to_all.133 = bf16[3,512,288]{2,0,1:T(4,128)(2,1)S(1)} all-to-all(bf16[3,512,288]{2,0,1:T(4,128)(2,1)S(1)} %copy.77), channel_id=1, replica_groups=mesh['seq'=4,'fsdp'=8] {'seq'}, dimensions={1} | all-to-all | bytes 1769472 | tf_op jit(solution)/shard_map/all_to_all | solution.py:285
  533.3 5.2 fusion.52
  538.6 2.8 copy.79
  541.4 20.5 %all_to_all.134 = bf16[3,512,288]{2,0,1:T(4,128)(2,1)S(1)} all-to-all(bf16[3,512,288]{2,0,1:T(4,128)(2,1)S(1)} %copy.79), channel_id=1, replica_groups=mesh['seq'=4,'fsdp'=8] {'seq'}, dimensions={1} | all-to-all | bytes 1769472 | tf_op jit(solution)/shard_map/all_to_all | solution.py:286
  564.7 5.2 fusion.53
  571.4 11.5 fusion.33
  584.1 15.7 %fusion.43 = f32[4304,1152]{1,0:T(8,128)} fusion(bf16[384,1152]{1,0:T(8,128)(2,1)S(1)} %bitcast.214, f32[384,4304]{0,1:T(8,128)} %get-tuple-element.275), kind=kOutput, calls=%fused_computation.126 | convolution fusion | flops 3822778368 | bytes 27328512 | tf_op jit(solution)/shard_map/dot_general | solution.py:29
  599.8 387.6 %fusion = f32[544,1152]{1,0:T(8,128)} fusion(f32[4304,1152]{1,0:T(8,128)} %fusion.43), kind=kCustom, calls=%all-reduce-scatter | all-reduce-scatter fusion | flops 5013505 | bytes 22340096
  991.7 9.9 concatenate.7
  1001.6 3.4 constant_dynamic-slice_fusion.8
  1005.0 45.8 %reduce-scatter.16.cloned.1.call-done = f32[144,4304]{1,0:T(8,128)} async-done(((f32[1152,4304]{1,0:T(8,128)}), f32[144,4304]{1,0:T(8,128)}) %reduce-scatter.16.cloned.1.call-update) | async-done | bytes 2479120 | tf_op jit(solution)/shard_map/reduce_scatter | solution.py:323
  1052.2 11.6 fusion.29
  1066.0 3.4 fusion.51
  1071.8 2.9 multiply_reduce_fusion.1
  1074.8 29.1 %all-reduce.20 = (f32[1152]{0:T(1024)S(1)}, f32[1152]{0:T(1024)S(1)}, f32[1152]{0:T(1024)S(1)}, f32[1152]{0:T(1024)S(1)}, f32[1152]{0:T(1024)S(1)}, /*index=5*/f...) all-reduce(f32[1152]{0:T(1024)S(1)} %get-tuple-element.175, ...), channel_id=2, replica_groups=mesh['seq'=4,'fsdp'=8] {'fsdp'}, use_global_device_ids=true, to_apply=%region_16.17.clone | all-reduce | flops 13520 | bytes 108160
  1104.6 17.3 %all-reduce.21 = (f32[144]{0:T(256)}, f32[144]{0:T(256)}, f32[144]{0:T(256)}, f32[144]{0:T(256)}, f32[144]{0:T(256)}, /*index=5*/f32[144]{0:T(256)}, f32[144]{0:T(256)}, f32[538]{0:T(1024)}, f32[144]{0:T(256)}) all-reduce(f32[144]{0:T(256)S(1)} %dynamic-slice.10, ...), channel_id=1, replica_groups=mesh['seq'=4,'fsdp'=8] {'seq'}, use_global_device_ids=true, to_apply=%region_17.18 | all-reduce | flops 1690 | bytes 13520 | tf_op jit(solution)/shard_map/psum | solution.py:328
  1121.8 3.3 multiply_add_fusion
  1125.1 92.1 %all-reduce.26.cloned.1.call-done = (f32[144,1152]{1,0:T(8,128)}, f32[144,1152]{1,0:T(8,128)}, f32[144,1152]{1,0:T(8,128)}, f32[144,1152]{1,0:T(8,128)}, f32[144,4304]{1,0:T(8,128)}, /*index=5*/f32[538,1152]{1,0:T(8,128)}) async-done(((f32[144,1152]{1,0:T(8,128)}, f32[144,1152]{1,0:T(8,128)}, f32[144,1152]{1,0:T(8,128)}, f32[144,1152]{1,0:T(8,128)}, f32[144,4304]{1,0:T(8,128)}, ...) | async-done | bytes 7612432 | tf_op jit(solution)/shard_map/psum | solution.py:328
  (334 shorter events, 120.2 us)
Async XLA Ops:
  7.2 81.5 %copy-start.52 = (u32[32]{0:T(128)S(1)}, u32[32]{0:T(128)}, u32[]{:S(2)}) copy-start(u32[32]{0:T(128)} %constant.144) | copy-start | bytes 388
  7.2 77.5 %copy-start = (bf16[3,128,1152]{2,1,0:T(8,128)(2,1)S(1)}, bf16[3,128,1152]{2,1,0:T(8,128)(2,1)}, u32[]{:S(2)}) copy-start(bf16[3,128,1152]{2,1,0:T(8,128)(2,1)} %param.22) | copy-start | bytes 2654212
  7.2 83.4 %copy-start.57 = (bf16[144]{0:T(256)(128)(2,1)S(1)}, bf16[144]{0:T(256)(128)(2,1)}, u32[]{:S(2)}) copy-start(bf16[144]{0:T(256)(128)(2,1)} %param.24) | copy-start | bytes 868
  7.2 83.7 %copy-start.58 = (bf16[144]{0:T(256)(128)(2,1)S(1)}, bf16[144]{0:T(256)(128)(2,1)}, u32[]{:S(2)}) copy-start(bf16[144]{0:T(256)(128)(2,1)} %param.30) | copy-start | bytes 868
  7.2 83.9 %copy-start.59 = (bf16[144]{0:T(256)(128)(2,1)S(1)}, bf16[144]{0:T(256)(128)(2,1)}, u32[]{:S(2)}) copy-start(bf16[144]{0:T(256)(128)(2,1)} %param.29) | copy-start | bytes 868
  7.2 84.1 %copy-start.60 = (bf16[144]{0:T(256)(128)(2,1)S(1)}, bf16[144]{0:T(256)(128)(2,1)}, u32[]{:S(2)}) copy-start(bf16[144]{0:T(256)(128)(2,1)} %param.32) | copy-start | bytes 868
  7.3 84.4 %copy-start.61 = (bf16[144]{0:T(256)(128)(2,1)S(1)}, bf16[144]{0:T(256)(128)(2,1)}, u32[]{:S(2)}) copy-start(bf16[144]{0:T(256)(128)(2,1)} %param.33) | copy-start | bytes 868
  7.3 84.6 %copy-start.62 = (bf16[144]{0:T(256)(128)(2,1)S(1)}, bf16[144]{0:T(256)(128)(2,1)}, u32[]{:S(2)}) copy-start(bf16[144]{0:T(256)(128)(2,1)} %param.34) | copy-start | bytes 868
  7.3 84.9 %copy-start.63 = (bf16[144]{0:T(256)(128)(2,1)S(1)}, bf16[144]{0:T(256)(128)(2,1)}, u32[]{:S(2)}) copy-start(bf16[144]{0:T(256)(128)(2,1)} %param.38) | copy-start | bytes 868
  7.3 85.1 %copy-start.64 = (bf16[144]{0:T(256)(128)(2,1)S(1)}, bf16[144]{0:T(256)(128)(2,1)}, u32[]{:S(2)}) copy-start(bf16[144]{0:T(256)(128)(2,1)} %param.25) | copy-start | bytes 868
  7.3 85.4 %copy-start.54 = (bf16[538]{0:T(1024)(128)(2,1)S(1)}, bf16[538]{0:T(1024)(128)(2,1)}, u32[]{:S(2)}) copy-start(bf16[538]{0:T(1024)(128)(2,1)} %param.36) | copy-start | bytes 3232
  7.3 172.6 %all-gather.10.cloned.1.call-start = ((), (), s32[]{:S(2)}) async-start(), calls=%async_computation.14 | async-start | bytes 2985984 | tf_op jit(solution)/shard_map/all_gather | solution.py:158
  8.0 183.9 %all-gather.12.cloned.1.call-start = ((), (), s32[]{:S(2)}) async-start(), calls=%async_computation.15 | async-start | bytes 2985984 | tf_op jit(solution)/shard_map/all_gather | solution.py:159
  8.8 190.5 %all-gather.8.cloned.1.call-start = ((), (), s32[]{:S(2)}) async-start(), calls=%async_computation.13 | async-start | bytes 2985984 | tf_op jit(solution)/shard_map/all_gather | solution.py:160
  9.5 305.8 %all-gather.14.cloned.1.call-start = ((), (), s32[]{:S(2)}) async-start(), calls=%async_computation.16 | async-start | bytes 2985984 | tf_op jit(solution)/shard_map/all_gather | solution.py:163
  10.1 310.8 %all-gather.18.cloned.1.call-start = ((), (), s32[]{:S(2)}) async-start(), calls=%async_computation.23 | async-start | bytes 11280384 | tf_op jit(solution)/shard_map/all_gather | solution.py:169
  10.7 163.8 %copy-start.49 = (s32[3,512]{1,0:T(4,128)S(1)}, s32[3,512]{1,0:T(4,128)}, u32[]{:S(2)}) copy-start(s32[3,512]{1,0:T(4,128)} %param.23) | copy-start | bytes 18436
  10.7 382.1 %all-gather.16.cloned.1.call-start = ((), (), s32[]{:S(2)}) async-start(), calls=%async_computation.17 | async-start | bytes 11280384 | tf_op jit(solution)/shard_map/all_gather | solution.py:234
  10.7 30.6 %collective-permute-start = (bf16[144,4304]{1,0:T(8,128)(2,1)}, bf16[144,4304]{1,0:T(8,128)(2,1)S(1)}, u32[]{:S(2)}, u32[]{:S(2)}) collective-permute-start(bf16[144,4304]{1,0:T(8,128)(2,1)} %param.35), channel_id=1, source_target_pairs={{0,1},{1,2},{2,3},{3,4},{4,5},{5,6},{6,7},{7,0},{8,9},{9,10},{10,1... | collective-permute-start | bytes 3718664 | tf_op jit(solution)/shard_map/ppermute | solution.py:17
  41.4 43.5 %copy-start.14 = (bf16[144,4304]{1,0:T(8,128)(2,1)}, bf16[144,4304]{1,0:T(8,128)(2,1)S(1)}, u32[]{:S(2)}) copy-start(bf16[144,4304]{1,0:T(8,128)(2,1)S(1)} %collective-permute-done) | copy-start | bytes 3718660
  41.4 30.4 %collective-permute-start.1 = (bf16[144,4304]{1,0:T(8,128)(2,1)S(1)}, bf16[144,4304]{1,0:T(8,128)(2,1)}, u32[]{:S(2)}, u32[]{:S(2)}) collective-permute-start(bf16[144,4304]{1,0:T(8,128)(2,1)S(1)} %collective-permute-done), channel_id=1, source_target_pairs={{0,1},{1,2},{2,3},{3,4},{4,5},{5,6},{6,7},{7,0},{8,9},{9,10},{10,1... | collective-permute-start | bytes 3718664 | tf_op jit(solution)/shard_map/ppermute | solution.py:17
  43.0 42.1 %collective-permute-start.4 = (bf16[144,4304]{1,0:T(8,128)(2,1)}, bf16[144,4304]{1,0:T(8,128)(2,1)S(1)}, u32[]{:S(2)}, u32[]{:S(2)}) collective-permute-start(bf16[144,4304]{1,0:T(8,128)(2,1)} %param.35), channel_id=1, source_target_pairs={{0,7},{1,0},{2,1},{3,2},{4,3},{5,4},{6,5},{7,6},{8,15},{9,8},{10,9... | collective-permute-start | bytes 3718664 | tf_op jit(solution)/shard_map/ppermute | solution.py:19
  71.8 102.6 %collective-permute-start.2 = (bf16[144,4304]{1,0:T(8,128)(2,1)}, bf16[144,4304]{1,0:T(8,128)(2,1)}, u32[]{:S(2)}, u32[]{:S(2)}) collective-permute-start(bf16[144,4304]{1,0:T(8,128)(2,1)} %collective-permute-done.1), channel_id=1, source_target_pairs={{0,1},{1,2},{2,3},{3,4},{4,5},{5,6},{6,7},{7,0},{8,9},{9,10},{10,1... | collective-permute-start | bytes 3718664 | tf_op jit(solution)/shard_map/ppermute | solution.py:17
  85.0 99.3 %copy-start.11 = (bf16[144,4304]{1,0:T(8,128)(2,1)}, bf16[144,4304]{1,0:T(8,128)(2,1)S(1)}, u32[]{:S(2)}) copy-start(bf16[144,4304]{1,0:T(8,128)(2,1)S(1)} %collective-permute-done.4) | copy-start | bytes 3718660
  85.0 91.3 %collective-permute-start.5 = (bf16[144,4304]{1,0:T(8,128)(2,1)S(1)}, bf16[144,4304]{1,0:T(8,128)(2,1)S(1)}, u32[]{:S(2)}, u32[]{:S(2)}) collective-permute-start(bf16[144,4304]{1,0:T(8,128)(2,1)S(1)} %collective-permute-done.4), channel_id=1, source_target_pairs={{0,7},{1,0},{2,1},{3,2},{4,3},{5,4},{6,5},{7,6},{8,15},{9,8},{10,9... | collective-permute-start | bytes 3718664 | tf_op jit(solution)/shard_map/ppermute | solution.py:19
  88.7 95.6 %copy-start.42 = (f32[384]{0:T(512)}, f32[384]{0:T(512)S(1)}, u32[]{:S(2)}) copy-start(f32[384]{0:T(512)S(1)} %get-tuple-element.268) | copy-start | bytes 4612
  88.7 95.6 %copy-start.46 = (f32[3,128]{1,0:T(4,128)}, f32[3,128]{1,0:T(4,128)S(1)}, u32[]{:S(2)}) copy-start(f32[3,128]{1,0:T(4,128)S(1)} %get-tuple-element.269) | copy-start | bytes 4612
  173.2 11.2 copy-start.44
  174.5 44.0 %collective-permute-start.3 = (bf16[144,4304]{1,0:T(8,128)(2,1)}, bf16[144,4304]{1,0:T(8,128)(2,1)}, u32[]{:S(2)}, u32[]{:S(2)}) collective-permute-start(bf16[144,4304]{1,0:T(8,128)(2,1)} %collective-permute-done.2), channel_id=1, source_target_pairs={{0,1},{1,2},{2,3},{3,4},{4,5},{5,6},{6,7},{7,0},{8,9},{9,10},{10,1... | collective-permute-start | bytes 3718664 | tf_op jit(solution)/shard_map/ppermute | solution.py:17
  176.4 53.2 %copy-start.10 = (bf16[144,4304]{1,0:T(8,128)(2,1)}, bf16[144,4304]{1,0:T(8,128)(2,1)S(1)}, u32[]{:S(2)}) copy-start(bf16[144,4304]{1,0:T(8,128)(2,1)S(1)} %collective-permute-done.5) | copy-start | bytes 3718660
  176.4 54.4 %collective-permute-start.6 = (bf16[144,4304]{1,0:T(8,128)(2,1)S(1)}, bf16[144,4304]{1,0:T(8,128)(2,1)}, u32[]{:S(2)}, u32[]{:S(2)}) collective-permute-start(bf16[144,4304]{1,0:T(8,128)(2,1)S(1)} %collective-permute-done.5), channel_id=1, source_target_pairs={{0,7},{1,0},{2,1},{3,2},{4,3},{5,4},{6,5},{7,6},{8,15},{9,8},{10,9... | collective-permute-start | bytes 3718664 | tf_op jit(solution)/shard_map/ppermute | solution.py:19
  184.3 7.6 copy-start.25
  187.6 50.5 %all-to-all-start.1 = ((bf16[3,128,1152]{1,0,2:T(4,128)(2,1)}), bf16[3,128,1152]{1,0,2:T(4,128)(2,1)}, u32[]{:S(2)}, u32[]{:S(2)}) async-start(bf16[3,128,1152]{1,0,2:T(4,128)(2,1)} %copy.66), calls=%async_computation.1 | async-start | bytes 2359296 | tf_op jit(solution)/shard_map/all_to_all | solution.py:200
  221.0 5.2 copy-start.15
  238.2 6.8 copy-start.16
  238.2 19.3 %all-to-all-start = ((bf16[3,128,1152]{1,0,2:T(4,128)(2,1)}), bf16[3,128,1152]{1,0,2:T(4,128)(2,1)}, u32[]{:S(2)}, u32[]{:S(2)}) async-start(bf16[3,128,1152]{1,0,2:T(4,128)(2,1)} %copy.63), calls=%async_computation | async-start | bytes 2359296 | tf_op jit(solution)/shard_map/all_to_all | solution.py:206
  246.1 17.2 %copy-start.13 = (bf16[144,4304]{1,0:T(8,128)(2,1)S(1)}, bf16[144,4304]{1,0:T(8,128)(2,1)}, u32[]{:S(2)}) copy-start(bf16[144,4304]{1,0:T(8,128)(2,1)} %copy-done.11) | copy-start | bytes 3718660
  257.5 14.9 %all-to-all-start.2 = ((bf16[3,128,1152]{1,0,2:T(4,128)(2,1)}), bf16[3,128,1152]{1,0,2:T(4,128)(2,1)}, u32[]{:S(2)}, u32[]{:S(2)}) async-start(bf16[3,128,1152]{1,0,2:T(4,128)(2,1)} %copy.69), calls=%async_computation.2 | async-start | bytes 2359296 | tf_op jit(solution)/shard_map/all_to_all | solution.py:203
  292.3 16.7 %all-to-all-start.3 = ((bf16[3,512,288]{2,0,1:T(4,128)(2,1)}), bf16[3,512,288]{2,0,1:T(4,128)(2,1)}, u32[]{:S(2)}, u32[]{:S(2)}) async-start(bf16[3,512,288]{2,0,1:T(4,128)(2,1)} %copy.72), calls=%async_computation.3 | async-start | bytes 3145728 | tf_op jit(solution)/shard_map/all_to_all | solution.py:212
  296.6 708.3 %reduce-scatter.14.cloned.1.call-start = ((), (), s32[]{:S(2)}) async-start(), calls=%async_computation.21 | async-start | bytes 5971968 | tf_op jit(solution)/shard_map/reduce_scatter | solution.py:319
  332.8 9.1 copy-start.2
  332.8 9.1 copy-start.31
  332.8 9.1 copy-start.35
  332.8 9.1 copy-start.40
  392.8 11.1 copy-start.3
  392.8 11.1 copy-start.8
  392.8 11.1 copy-start.36
  470.5 7.0 copy-start.29
  470.5 7.0 copy-start.34
  470.5 7.0 copy-start.47
  470.5 7.0 copy-start.48
  473.9 22.2 %all-to-all-start.7 = ((bf16[3,512,288]{2,0,1:T(4,128)(2,1)}), bf16[3,512,288]{2,0,1:T(4,128)(2,1)S(1)}, u32[]{:S(2)}, u32[]{:S(2)}) async-start(bf16[3,512,288]{2,0,1:T(4,128)(2,1)} %copy.81), calls=%async_computation.7 | async-start | bytes 3145728 | tf_op jit(solution)/shard_map/all_to_all | solution.py:287
  477.5 527.5 %reduce-scatter.12.cloned.1.call-start = ((), (), s32[]{:S(2)}) async-start(), calls=%async_computation.20 | async-start | bytes 5971968 | tf_op jit(solution)/shard_map/reduce_scatter | solution.py:316
  501.0 4.0 copy-start.18
  505.1 499.9 %reduce-scatter.8.cloned.1.call-start = ((), (), s32[]{:S(2)}) async-start(), calls=%async_computation.18 | async-start | bytes 5971968 | tf_op jit(solution)/shard_map/reduce_scatter | solution.py:314
  538.5 466.5 %reduce-scatter.10.cloned.1.call-start = ((), (), s32[]{:S(2)}) async-start(), calls=%async_computation.19 | async-start | bytes 5971968 | tf_op jit(solution)/shard_map/reduce_scatter | solution.py:315
  569.9 480.9 %reduce-scatter.16.cloned.1.call-start = ((), (), s32[]{:S(2)}) async-start(), calls=%async_computation.22 | async-start | bytes 22560768 | tf_op jit(solution)/shard_map/reduce_scatter | solution.py:323
  583.0 634.3 %all-reduce.26.cloned.1.call-start = ((), (), s32[]{:S(2)}) async-start(), calls=%async_computation.24 | async-start | bytes 15335424 | tf_op jit(solution)/shard_map/psum | solution.py:328
  989.0 2.7 collective-permute-start.7
  1052.2 13.8 %copy-start.20 = (bf16[384,1152]{1,0:T(8,128)(2,1)S(1)}, bf16[384,1152]{1,0:T(8,128)(2,1)}, u32[]{:S(2)}) copy-start(bf16[384,1152]{1,0:T(8,128)(2,1)} %reshape.284) | copy-start | bytes 2654212
  1071.8 50.0 %copy-start.6 = (f32[384,1152]{1,0:T(8,128)S(1)}, f32[384,1152]{1,0:T(8,128)}, u32[]{:S(2)}) copy-start(f32[384,1152]{1,0:T(8,128)} %copy-done.5) | copy-start | bytes 5308420
  1217.2 4.1 copy-start.27
  1217.2 4.9 copy-start.26
  1217.2 5.8 copy-start.24
  (26 other events, 56.9 us)
Sparse Core Ops, SparseCore 0:
  9.8 45.9 all-gather.9
  57.4 49.1 all-gather.11
  108.3 42.0 all-gather.7
  151.9 41.8 all-gather.13
  195.3 101.3 all-gather.17
  298.2 94.5 all-gather.15
  410.6 58.8 reduce-scatter.13
  505.2 57.8 reduce-scatter.11
  565.4 74.5 reduce-scatter.7
  642.1 111.4 reduce-scatter.9
  756.0 294.6 reduce-scatter.15
  1055.6 161.5 all-reduce.25
